TPU v7x, 32 devices: a whole 2x2x4 slice. The times are simulated.
32 devices in a mesh: seq: 8 (over z, y), tp: 4 (over x, core).
Axes of the slice: x: 2, y: 2, z: 4, core: 2. Of those that a mesh axis runs over, the one named last changes fastest.
Arguments:
- query: bfloat16 [4096, 8192], P('seq', 'tp'), may hold values from -6 to 6
- key: bfloat16 [4096, 8192], P('seq', 'tp'), may hold values from -6 to 6
- value: bfloat16 [4096, 8192], P('seq', 'tp'), may hold values from -6 to 6
- gain: float32 [8192], P('tp'), may hold values from 0.1 to 1.9
- cotangent: bfloat16 [4096, 8192], P('seq', 'tp'), may hold values from -24 to 24
Outputs:
- normed: bfloat16 [4096, 8192], P('seq', 'tp')
- grad_query: bfloat16 [4096, 8192], P('seq', 'tp')
- grad_key: bfloat16 [4096, 8192], P('seq', 'tp')
- grad_value: bfloat16 [4096, 8192], P('seq', 'tp')
- grad_gain: float32 [8192], P('tp')
All inputs are finite; a program needn't handle non-finite values.
Results may differ from a plain program's by a relative error of at most 0.013.
Values may be sent and summed in bfloat16 or wider, within the bound.
A program may use at most 128 MiB of HBM per device.

v0:
```python
import jax
import jax.numpy as jnp
from jax import lax
from jax.sharding import PartitionSpec as P

HEADS = 64
HD = 128


epsilon = 1e-06


def local(query, key, value, gain, cotangent):
    rows_here, local_width = query.shape
    head_count = local_width // HD
    full_width = HEADS * HD
    block_rows = min(rows_here, 512)
    blocks = rows_here // block_rows
    queries = query.reshape(rows_here, head_count, HD)
    keys_all = key.reshape(rows_here, head_count, HD)
    values_all = value.reshape(rows_here, head_count, HD)
    own_index = lax.axis_index("seq")
    key_rows = jnp.arange(rows_here)
    local_kv = jnp.einsum(
        "thd,the->hde", keys_all, values_all, preferred_element_type=jnp.float32
    ).astype(jnp.bfloat16)
    shard_rows = lax.all_gather(local_kv[None], "seq", axis=0, tiled=True)
    owners = jnp.arange(shard_rows.shape[0])
    weight = (owners < own_index).astype(jnp.float32)
    prefix = jnp.sum(weight[:, None, None, None] * shard_rows.astype(jnp.float32), axis=0)
    prefix_low = prefix.astype(jnp.bfloat16)

    def forward_block(block_index):
        first_row = block_index * block_rows
        causal = (first_row + jnp.arange(block_rows))[:, None] >= key_rows[None, :]
        scores = jnp.einsum("thd,shd->hts", queries, keys_all, preferred_element_type=jnp.float32)
        scores_low = jnp.where(causal[None], scores, 0.0).astype(jnp.bfloat16)
        attended = jnp.einsum(
            "hts,shd->thd", scores_low, values_all, preferred_element_type=jnp.float32
        )
        attended = attended + jnp.einsum(
            "thd,hde->the", queries, prefix_low, preferred_element_type=jnp.float32
        )
        return (scores_low, attended)

    score_blocks, attended_blocks = lax.map(forward_block, jnp.arange(blocks))
    attended = attended_blocks.reshape(rows_here, local_width)
    grad_f = cotangent.astype(jnp.float32)
    scaled_grad = grad_f * gain
    squares, cross = lax.psum(
        (jnp.sum(attended * attended, axis=1), jnp.sum(attended * scaled_grad, axis=1)), "tp"
    )
    inverse = lax.rsqrt(squares / full_width + epsilon)
    normed = (attended * inverse[:, None] * gain).astype(jnp.bfloat16)
    grad_out = (
        scaled_grad * inverse[:, None] - attended * (inverse**3 * cross / full_width)[:, None]
    )
    grad_out = grad_out.astype(jnp.bfloat16).reshape(rows_here, head_count, HD)
    gain_part = jnp.sum(grad_f * attended * inverse[:, None], axis=0)
    grad_gain = lax.psum(gain_part, "seq")
    local_qg = jnp.einsum(
        "thd,the->hde", queries, grad_out, preferred_element_type=jnp.float32
    ).astype(jnp.bfloat16)
    shard_rows = lax.all_gather(local_qg[None], "seq", axis=0, tiled=True)
    owners = jnp.arange(shard_rows.shape[0])
    weight = (owners > own_index).astype(jnp.float32)
    suffix = jnp.sum(weight[:, None, None, None] * shard_rows.astype(jnp.float32), axis=0)
    suffix_low = suffix.astype(jnp.bfloat16)

    def backward_block(totals, inputs):
        block_index, scores_low = inputs
        key_total, value_total = totals
        first_row = block_index * block_rows
        causal = (first_row + jnp.arange(block_rows))[:, None] >= key_rows[None, :]
        back = jnp.einsum("thd,shd->hts", grad_out, values_all, preferred_element_type=jnp.float32)
        back_low = jnp.where(causal[None], back, 0.0).astype(jnp.bfloat16)
        grad_q = jnp.einsum("hts,shd->thd", back_low, keys_all, preferred_element_type=jnp.float32)
        grad_q = grad_q + jnp.einsum(
            "the,hde->thd", grad_out, prefix_low, preferred_element_type=jnp.float32
        )
        key_total = key_total + jnp.einsum(
            "hts,thd->shd", back_low, queries, preferred_element_type=jnp.float32
        )
        value_total = value_total + jnp.einsum(
            "hts,the->she", scores_low, grad_out, preferred_element_type=jnp.float32
        )
        return ((key_total, value_total), grad_q.astype(jnp.bfloat16))

    zero_rows = jnp.zeros((rows_here, head_count, HD), jnp.float32)
    (key_total, value_total), grad_q_blocks = lax.scan(
        backward_block, (zero_rows, zero_rows), (jnp.arange(blocks), score_blocks)
    )
    grad_k = key_total + jnp.einsum(
        "she,hde->shd", values_all, suffix_low, preferred_element_type=jnp.float32
    )
    grad_v = value_total + jnp.einsum(
        "shd,hde->she", keys_all, suffix_low, preferred_element_type=jnp.float32
    )
    return (
        normed,
        grad_q_blocks.reshape(rows_here, local_width),
        grad_k.astype(jnp.bfloat16).reshape(rows_here, local_width),
        grad_v.astype(jnp.bfloat16).reshape(rows_here, local_width),
        grad_gain,
    )


def solution(mesh):
    return jax.shard_map(
        local,
        mesh=mesh,
        in_specs=(P("seq", "tp"), P("seq", "tp"), P("seq", "tp"), P("tp"), P("seq", "tp")),
        out_specs=(P("seq", "tp"), P("seq", "tp"), P("seq", "tp"), P("seq", "tp"), P("tp")),
        check_vma=False,
    )
```

profile of v0, /device:TPU:0, one launch (start us, length us, event | category | flops | bytes accessed | tf_op | source)
XLA Modules:
  0.0 239.6 jit_solution(4980517580974492038)
XLA Ops:
  7.2 0.0 copy-start
  7.2 0.0 all-gather.5.cloned.1.call-start
  7.2 3.7 %copy.93 = bf16[64,8,16,128]{3,2,1,0:T(8,128)(2,1)} copy(bf16[64,8,16,128]{3,1,2,0:T(8,128)(2,1)} %bitcast.114) | data formatting | bytes 4194304
  10.9 4.3 %copy.64 = bf16[512,16,128]{0,2,1:T(8,128)(2,1)} copy(bf16[512,16,128]{2,1,0:T(8,128)(2,1)} %bitcast.117) | data formatting | bytes 4194304 | tf_op jit(solution)/shard_map/reshape | solution.py:20
  15.2 3.7 %fusion.38 = bf16[16,128,128]{2,1,0:T(8,128)(2,1)} fusion(bf16[512,16,128]{0,2,1:T(8,128)(2,1)} %copy.64, bf16[512,2048]{1,0:T(8,128)(2,1)} %param.7), kind=kOutput, calls=%fused_computation.48 | convolution fusion | flops 268697600 | bytes 4718592 | tf_op jit(solution)/shard_map/thd,the->hde/dot_general | solution.py:24
  18.9 0.0 all-gather.5.cloned.1.call-update
  18.9 0.0 all-gather.7.cloned.1.call-start
  19.0 0.1 iota_compare_fusion
  19.1 0.0 copy-done
  19.1 0.0 copy-start.6
  19.1 4.1 %select_convert_fusion.1 = bf16[16,512,512]{2,1,0:T(8,128)(2,1)S(1)} fusion(pred[512,512]{1,0:T(8,128)(4,1)S(1)} %iota_compare_fusion, bf16[512,2048]{1,0:T(8,128)(2,1)} %param.6, bf16[512,2048]{1,0:T(8,128)(2,1)S(1)} %copy-done), kind=kOutput, calls=%fused_computation.1 | convolution fusion | flops 1082130432 | bytes 12845056 | tf_op jit(solution)/shard_map/while/body/eval_jaxpr/thd,shd->hts/dot_general | solution.py:36
  23.3 0.0 copy-start.1
  23.3 3.2 %copy-done.1 = bf16[16,512,512]{2,1,0:T(8,128)(2,1)} copy-done((bf16[16,512,512]{2,1,0:T(8,128)(2,1)}, bf16[16,512,512]{2,1,0:T(8,128)(2,1)S(1)}, u32[]{:S(2)}) %copy-start.1) | copy-done | bytes 8388632
  26.5 4.8 %fusion.11 = f32[16,512,128]{1,2,0:T(8,128)} fusion(bf16[16,512,512]{2,1,0:T(8,128)(2,1)S(1)} %select_convert_fusion.1, bf16[512,2048]{1,0:T(8,128)(2,1)S(1)} %copy-done.6), kind=kOutput, calls=%fused_computation.23 | convolution fusion | flops 1073741824 | bytes 14680064 | tf_op jit(solution)/shard_map/while/body/eval_jaxpr/hts,shd->thd/dot_general | solution.py:38
  31.3 63.3 %all-gather.5.cloned.1.call-done = bf16[128,128,128]{2,1,0:T(8,128)(2,1)} async-done(((bf16[16,128,128]{2,1,0:T(8,128)(2,1)}), bf16[128,128,128]{2,1,0:T(8,128)(2,1)}) %all-gather.5.cloned.1.call-update) | async-done | bytes 4194320 | tf_op jit(solution)/shard_map/all_gather | solution.py:27
  94.6 3.3 %fusion.1 = bf16[16,128,128]{2,1,0:T(8,128)(2,1)S(1)} fusion(bf16[8,16,128,128]{3,2,1,0:T(8,128)(2,1)} %bitcast.120, f32[8]{0:T(128)S(1)} %compare_convert_fusion.1), kind=kLoop, calls=%fused_computation.5 | loop fusion | flops 6029312 | bytes 4718624 | tf_op jit(solution)/shard_map/reduce_sum | solution.py:30
  97.9 0.2 copy-done.5
  98.1 2.9 %multiply_reduce_fusion = (f32[512]{0:T(512)S(1)}, f32[512,16,128]{0,2,1:T(8,128)}) fusion(bf16[16,128,128]{2,1,0:T(8,128)(2,1)S(1)} %fusion.1, f32[16,512,128]{1,2,0:T(8,128)S(1)} %copy-done.5, bf16[512,2048]{1,0:T(8,128)(2,1)S(1)} %copy-done), kind=kOutput, calls=%fused_computation.22 | convolution fusion | flops 271580672 | bytes 11012096 | tf_op jit(solution)/shard_map/while/body/eval_jaxpr/thd,hde->the/dot_general | solution.py:41
  101.0 5.6 %psum.21 = f32[512]{0:T(512)S(1)} all-reduce(f32[512]{0:T(512)S(1)} %get-tuple-element.81), channel_id=1, replica_groups=mesh['seq'=8,'tp'=4] {'tp'}, use_global_device_ids=true, to_apply=%region_2.3 | all-reduce | flops 512 | bytes 4096 | tf_op jit(solution)/shard_map/psum | solution.py:50
  106.6 5.4 %copy.68 = f32[512,2048]{1,0:T(8,128)} copy(f32[512,2048]{0,1:T(8,128)} %bitcast.113) | data formatting | bytes 8388608 | tf_op jit(solution)/shard_map/reshape | solution.py:47
  112.0 4.2 %fusion.8 = (f32[2048]{0:T(1024)S(1)}, f32[512]{0:T(512)S(1)}) fusion(f32[512,2048]{1,0:T(8,128)} %copy.68, bf16[512,2048]{1,0:T(8,128)(2,1)} %param.9, f32[512]{0:T(512)S(1)} %add_rsqrt_fusion, f32[2048]{0:T(1024)S(1)} %copy-done.10), kind=kLoop, calls=%fused_computation.14 | loop fusion | flops 7337472 | bytes 6311936 | tf_op jit(solution)/shard_map/reduce_sum | solution.py:59
  116.1 6.8 %psum.22 = f32[512]{0:T(512)S(1)} all-reduce(f32[512]{0:T(512)S(1)} %get-tuple-element.78), channel_id=1, replica_groups=mesh['seq'=8,'tp'=4] {'tp'}, use_global_device_ids=true, to_apply=%region_4.5 | all-reduce | flops 512 | bytes 4096 | tf_op jit(solution)/shard_map/psum | solution.py:50
  122.9 6.4 %fusion.5 = (bf16[512,2048]{1,0:T(8,128)(2,1)}, bf16[512,2048]{1,0:T(8,128)(2,1)}) fusion(bf16[512,2048]{1,0:T(8,128)(2,1)} %param.9, f32[512,2048]{1,0:T(8,128)} %copy.68, f32[512]{0:T(512)S(1)} %fusion.49, f32[2048]{0:T(1024)S(1)} %copy-done.10, f32[512]{0:T(512)S(1)} %add_rsqrt_fusion), kind=kLoop, calls=%fused_computation.11 | loop fusion | flops 9437184 | bytes 10498048 | tf_op jit(solution)/shard_map/convert_element_type | solution.py:58
  129.3 3.9 %copy.89 = bf16[512,2048]{0,1:T(8,128)(2,1)} copy(bf16[512,2048]{1,0:T(8,128)(2,1)} %get-tuple-element.79) | data formatting | bytes 4194304 | tf_op jit(solution)/shard_map/reshape | solution.py:58
  133.2 2.3 fusion.41
  135.5 1.0 copy.78
  136.6 0.0 all-gather.7.cloned.1.call-update
  136.6 0.0 copy-start.9
  136.6 4.9 %select_convert_fusion = bf16[16,512,512]{2,1,0:T(8,128)(2,1)S(1)} fusion(bf16[512,16,128]{0,2,1:T(8,128)(2,1)} %bitcast.110, pred[512,512]{1,0:T(8,128)(4,1)S(1)} %iota_compare_fusion, bf16[512,2048]{1,0:T(8,128)(2,1)} %param.7), kind=kOutput, calls=%fused_computation | convolution fusion | flops 1082130432 | bytes 12845056 | tf_op jit(solution)/shard_map/while/body/eval_jaxpr/thd,shd->hts/dot_general | solution.py:75
  141.5 0.0 copy-done.9
  141.5 0.0 copy-start.2
  141.5 0.0 copy-start.4
  141.5 4.8 %fusion.50 = f32[16,512,128]{1,2,0:T(8,128)} fusion(bf16[16,512,512]{2,1,0:T(8,128)(2,1)S(1)} %select_convert_fusion, bf16[512,16,128]{0,2,1:T(8,128)(2,1)S(1)} %copy-done.9), kind=kOutput, calls=%fused_computation.61 | convolution fusion | flops 1073741824 | bytes 14680064 | tf_op jit(solution)/shard_map/while/body/eval_jaxpr/hts,shd->thd/dot_general | solution.py:77
  146.3 0.1 copy-done.2
  146.4 4.3 %fusion.10 = bf16[512,16,128]{0,2,1:T(8,128)(2,1)} fusion(f32[16,512,128]{1,2,0:T(8,128)} %fusion.50, bf16[512,16,128]{0,2,1:T(8,128)(2,1)S(1)} %bitcast.112, bf16[16,128,128]{2,1,0:T(8,128)(2,1)S(1)} %fusion.1), kind=kOutput, calls=%fused_computation.18 | convolution fusion | flops 270532608 | bytes 8912896 | tf_op jit(solution)/shard_map/while/body/eval_jaxpr/the,hde->thd/dot_general | solution.py:78
  150.7 3.9 %copy.84 = bf16[512,2048]{1,0:T(8,128)(2,1)} copy(bf16[512,2048]{0,1:T(8,128)(2,1)} %bitcast.115) | data formatting | bytes 4194304
  154.6 20.9 %psum.23 = f32[2048]{0:T(1024)} all-reduce(f32[2048]{0:T(1024)S(1)} %get-tuple-element.77), channel_id=1, replica_groups=mesh['seq'=8,'tp'=4] {'seq'}, use_global_device_ids=true, to_apply=%region_7.8 | all-reduce | flops 2048 | bytes 16384 | tf_op jit(solution)/shard_map/psum | solution.py:60
  175.5 7.3 %fusion.51 = f32[16,128,512]{2,1,0:T(8,128)} fusion(bf16[512,16,128]{0,2,1:T(8,128)(2,1)} %bitcast.111, bf16[16,512,512]{2,1,0:T(8,128)(2,1)} %copy-done.1), kind=kOutput, calls=%fused_computation.62 | convolution fusion | flops 1073741824 | bytes 14680064 | tf_op jit(solution)/shard_map/while/body/eval_jaxpr/hts,the->she/dot_general | solution.py:84
  182.8 25.1 %all-gather.7.cloned.1.call-done = bf16[128,128,128]{2,1,0:T(8,128)(2,1)} async-done(((bf16[16,128,128]{2,1,0:T(8,128)(2,1)}), bf16[128,128,128]{2,1,0:T(8,128)(2,1)}) %all-gather.7.cloned.1.call-update) | async-done | bytes 4194320 | tf_op jit(solution)/shard_map/all_gather | solution.py:64
  207.8 3.3 %fusion = bf16[16,128,128]{2,1,0:T(8,128)(2,1)S(1)} fusion(bf16[8,16,128,128]{3,2,1,0:T(8,128)(2,1)} %bitcast.119, f32[8]{0:T(128)S(1)} %compare_convert_fusion), kind=kLoop, calls=%fused_computation.3 | loop fusion | flops 6029312 | bytes 4718624 | tf_op jit(solution)/shard_map/reduce_sum | solution.py:67
  211.1 0.0 copy-start.8
  211.1 2.9 %fusion.13 = f32[16,128,512]{2,1,0:T(8,128)} fusion(bf16[16,128,128]{2,1,0:T(8,128)(2,1)S(1)} %fusion, bf16[512,2048]{1,0:T(8,128)(2,1)S(1)} %copy-done.7), kind=kOutput, calls=%fused_computation.25 | convolution fusion | flops 268435456 | bytes 6815744 | tf_op jit(solution)/shard_map/she,hde->shd/dot_general | solution.py:93
  214.0 0.5 copy-done.3
  214.5 1.0 copy-done.8
  215.5 2.1 add_convert_fusion
  217.6 3.9 %copy.86 = bf16[512,2048]{1,0:T(8,128)(2,1)} copy(bf16[512,2048]{0,1:T(8,128)(2,1)} %bitcast.116) | data formatting | bytes 4194304
  221.5 7.4 %fusion.9 = bf16[512,16,128]{0,2,1:T(8,128)(2,1)} fusion(f32[16,128,512]{2,1,0:T(8,128)} %fusion.13, bf16[16,512,512]{2,1,0:T(8,128)(2,1)} %copy-done.2, bf16[512,2048]{1,0:T(8,128)(2,1)S(1)} %copy-done), kind=kOutput, calls=%fused_computation.16 | convolution fusion | flops 1075838976 | bytes 16777216 | tf_op jit(solution)/shard_map/while/body/eval_jaxpr/hts,thd->shd/dot_general | solution.py:81
  228.9 3.9 %copy.85 = bf16[512,2048]{1,0:T(8,128)(2,1)} copy(bf16[512,2048]{0,1:T(8,128)(2,1)} %bitcast.118) | data formatting | bytes 4194304
  (12 shorter events, 0.0 us)
Async XLA Ops:
  7.2 11.9 %copy-start = (bf16[512,2048]{1,0:T(8,128)(2,1)S(1)}, bf16[512,2048]{1,0:T(8,128)(2,1)}, u32[]{:S(2)}) copy-start(bf16[512,2048]{1,0:T(8,128)(2,1)} %param.5) | copy-start | bytes 6291460
  7.2 87.4 %all-gather.5.cloned.1.call-start = ((), (), s32[]{:S(2)}) async-start(), calls=%async_computation | async-start | bytes 4718592 | tf_op jit(solution)/shard_map/all_gather | solution.py:27
  18.9 188.9 %all-gather.7.cloned.1.call-start = ((), (), s32[]{:S(2)}) async-start(), calls=%async_computation.1 | async-start | bytes 4718592 | tf_op jit(solution)/shard_map/all_gather | solution.py:64
  19.1 7.4 %copy-start.6 = (bf16[512,2048]{1,0:T(8,128)(2,1)S(1)}, bf16[512,2048]{1,0:T(8,128)(2,1)}, u32[]{:S(2)}) copy-start(bf16[512,2048]{1,0:T(8,128)(2,1)} %param.7) | copy-start | bytes 6291460
  23.3 3.2 %copy-start.1 = (bf16[16,512,512]{2,1,0:T(8,128)(2,1)}, bf16[16,512,512]{2,1,0:T(8,128)(2,1)S(1)}, u32[]{:S(2)}) copy-start(bf16[16,512,512]{2,1,0:T(8,128)(2,1)S(1)} %select_convert_fusion.1) | copy-start | bytes 25165828
  94.6 3.4 %copy-start.5 = (f32[16,512,128]{1,2,0:T(8,128)S(1)}, f32[16,512,128]{1,2,0:T(8,128)}, u32[]{:S(2)}) copy-start(f32[16,512,128]{1,2,0:T(8,128)} %fusion.11) | copy-start | bytes 12582916
  106.6 5.4 %copy-start.10 = (f32[2048]{0:T(1024)S(1)}, f32[2048]{0:T(1024)}, u32[]{:S(2)}) copy-start(f32[2048]{0:T(1024)} %param.8) | copy-start | bytes 24580
  136.6 4.9 %copy-start.9 = (bf16[512,16,128]{0,2,1:T(8,128)(2,1)S(1)}, bf16[512,16,128]{0,2,1:T(8,128)(2,1)}, u32[]{:S(2)}) copy-start(bf16[512,16,128]{0,2,1:T(8,128)(2,1)} %copy.64) | copy-start | bytes 6291460
  141.5 4.9 %copy-start.2 = (bf16[16,512,512]{2,1,0:T(8,128)(2,1)}, bf16[16,512,512]{2,1,0:T(8,128)(2,1)S(1)}, u32[]{:S(2)}) copy-start(bf16[16,512,512]{2,1,0:T(8,128)(2,1)S(1)} %select_convert_fusion) | copy-start | bytes 25165828
  141.5 4.9 %copy-start.4 = (bf16[512,2048]{0,1:T(8,128)(2,1)S(1)}, bf16[512,2048]{0,1:T(8,128)(2,1)}, u32[]{:S(2)}) copy-start(bf16[512,2048]{0,1:T(8,128)(2,1)} %copy.89) | copy-start | bytes 6291460
  207.8 3.3 %copy-start.7 = (bf16[512,2048]{1,0:T(8,128)(2,1)S(1)}, bf16[512,2048]{1,0:T(8,128)(2,1)}, u32[]{:S(2)}) copy-start(bf16[512,2048]{1,0:T(8,128)(2,1)} %param.7) | copy-start | bytes 6291460
  211.1 3.4 %copy-start.3 = (f32[16,128,512]{2,1,0:T(8,128)S(1)}, f32[16,128,512]{2,1,0:T(8,128)}, u32[]{:S(2)}) copy-start(f32[16,128,512]{2,1,0:T(8,128)} %fusion.51) | copy-start | bytes 12582916
  211.1 4.4 %copy-start.8 = (bf16[512,2048]{1,0:T(8,128)(2,1)S(1)}, bf16[512,2048]{1,0:T(8,128)(2,1)}, u32[]{:S(2)}) copy-start(bf16[512,2048]{1,0:T(8,128)(2,1)} %param.6) | copy-start | bytes 6291460
Sparse Core Ops, SparseCore 0:
  19.1 75.5 all-gather.4
  136.7 71.0 all-gather.6
where the time goes:
time: 240 us
  waiting for transfers between devices  88.4 us (37%)
  matrix products  51.5 us (21%)
  local copies, waits for them, and re-layouts  35 us (15%)
  blocking collectives  33.3 us (14%)
  other arithmetic  17.2 us (7%)
  between operations  14.2 us (6%)
    all_gather x1, waiting for transfers between devices, local(): shard_rows = lax.all_gather(local_kv[None], 'seq', axis=0, tiled=True)  63.3 us
    all_gather x1, waiting for transfers between devices, local(): shard_rows = lax.all_gather(local_qg[None], 'seq', axis=0, tiled=True)  25.1 us
    psum x1, blocking collectives, local(): grad_gain = lax.psum(gain_part, 'seq')  20.9 us
    unnamed x26, local copies, waits for them, and re-layouts  20.4 us
    psum x2, blocking collectives, local(): lax.psum((jnp.sum(attended * attended, axis=1), jnp.sum(attended * scaled...  12.4 us
    dot_general x1, matrix products, backward_block(): jnp.einsum('hts,thd->shd', back_low, queries, preferred_element_type=jnp....  7.36 us
    dot_general x1, matrix products, backward_block(): jnp.einsum('hts,the->she', scores_low, grad_out, preferred_element_type=j...  7.3 us
    reduce_sum x2, other arithmetic, local(): jnp.sum(weight[:, None, None, None] * shard_rows.astype(jnp.float32), axi...  6.55 us
  transfers between devices with their start and end apart: 2, of which 2 were waited for; matrix products, arithmetic and copies ran while one was open for 14% of the time, Pallas kernels for 0%

commit v1 on v0

v1 whole, which is shorter than its diff:
```python
import functools

import jax
import jax.numpy as jnp
from jax import lax
from jax.experimental import pallas as pl
from jax.experimental.pallas import tpu as pltpu
from jax.sharding import PartitionSpec as P

HD = 128
epsilon = 1e-06
MESH = pl.DeviceIdType.MESH
F32 = jnp.float32
BF16 = jnp.bfloat16


def dot(a, b, ca, cb):
    return lax.dot_general(a, b, (((ca,), (cb,)), ((), ())), preferred_element_type=F32)


def kernel(
    n, ntp, inner, group, full_width,
    q_hbm, k_hbm, v_hbm, gain_ref, cot_hbm,
    normed_hbm, gq_hbm, gk_hbm, gv_hbm, gg_out,
    qb, kb, vb, cb, attb, goutb, gkb, gvb, nst, qst, kst, vst,
    fy, fzin, fzout, flow, by, bzin, bzout, blow,
    acc_sq, acc_cr, inv_b, coef_b, tpb, ggb,
    in_sem, out_sem,
    fys, fyr, fzs, fzr, bys, byr, bzs, bzr, tps, tpr, ggs, ggr,
):
    rows, width = qb.shape
    heads = width // HD
    chunks = heads // group
    outer = n // inner
    block = min(rows, 256)
    nblocks = rows // block
    me = lax.axis_index("seq")
    mt = lax.axis_index("tp")
    z = me // inner
    y = me % inner
    cw = group * HD

    def ccols(c):
        return pl.ds(pl.multiple_of(c * cw, cw), cw)

    def hcols(h):
        return pl.ds(pl.multiple_of(h * HD, HD), HD)

    ins = ((k_hbm, kb), (v_hbm, vb), (q_hbm, qb), (cot_hbm, cb))
    outs = ((nst, normed_hbm), (qst, gq_hbm), (kst, gk_hbm), (vst, gv_hbm))

    def in_copy(i, c):
        src, dst = ins[i]
        return pltpu.make_async_copy(src.at[:, ccols(c)], dst.at[:, ccols(c)], in_sem.at[i, c])

    def out_copy(i, c):
        src, dst = outs[i]
        return pltpu.make_async_copy(src.at[:, ccols(c)], dst.at[:, ccols(c)], out_sem.at[i, c])

    def loop(count, body):
        def step(i, carry):
            body(i)
            return carry
        lax.fori_loop(0, count, step, 0)

    def start_kv(c):
        in_copy(0, c).start()
        in_copy(1, c).start()

    def start_qc(c):
        in_copy(2, c).start()
        in_copy(3, c).start()

    loop(chunks, start_kv)
    loop(chunks, start_qc)

    barrier = pltpu.get_barrier_semaphore()

    def greet_seq(r):
        pl.semaphore_signal(barrier, inc=1, device_id={"seq": (me + 1 + r) % n}, device_id_type=MESH)

    def greet_tp(r):
        pl.semaphore_signal(barrier, inc=1, device_id={"tp": (mt + 1 + r) % ntp}, device_id_type=MESH)

    loop(n - 1, greet_seq)
    loop(ntp - 1, greet_tp)
    pl.semaphore_wait(barrier, n - 1 + ntp - 1)

    def row_send(c, r, buf, ssem, rsem):
        peer = (y + r) % inner
        return pltpu.make_async_remote_copy(
            src_ref=buf.at[y, c], dst_ref=buf.at[y, c],
            send_sem=ssem.at[peer, c], recv_sem=rsem.at[y, c],
            device_id={"seq": z * inner + peer}, device_id_type=MESH)

    def row_recv(c, r, buf, ssem, rsem):
        peer = (y + r) % inner
        return pltpu.make_async_remote_copy(
            src_ref=buf.at[peer, c], dst_ref=buf.at[peer, c],
            send_sem=ssem.at[peer, c], recv_sem=rsem.at[peer, c],
            device_id={"seq": z * inner + peer}, device_id_type=MESH)

    def chain(c, step, zin, zout, zs, zr):
        target = (me + step * inner + n) % n
        return pltpu.make_async_remote_copy(
            src_ref=zout.at[c], dst_ref=zin.at[c],
            send_sem=zs.at[c], recv_sem=zr.at[c],
            device_id={"seq": target}, device_id_type=MESH)

    def relay(c, step, buf, ys, yr, zin, zout, zs, zr, low, first, last):
        for r in range(1, inner):
            row_recv(c, r, buf, ys, yr).wait_recv()

        @pl.when(first)
        def _():
            zin[c] = jnp.zeros(zin.shape[1:], BF16)

        @pl.when(jnp.logical_not(first))
        def _():
            chain(c, step, zin, zout, zs, zr).wait_recv()

        @pl.when(jnp.logical_not(last))
        def _():
            total = zin[c].astype(F32)
            for other in range(inner):
                total = total + buf[other, c].astype(F32)
            zout[c] = total.astype(BF16)
            chain(c, step, zin, zout, zs, zr).start()

        mine = zin[c].astype(F32)
        for other in range(inner):
            before = (other < y) if step > 0 else (other > y)
            mine = mine + buf[other, c].astype(F32) * before.astype(F32)
        low[c] = mine.astype(BF16)

    def forward_state(c):
        in_copy(0, c).wait()
        in_copy(1, c).wait()
        for g in range(group):
            cols = hcols(c * group + g)
            fy[y, c, g] = dot(kb[:, cols], vb[:, cols], 0, 0).astype(BF16)
        for r in range(1, inner):
            row_send(c, r, fy, fys, fyr).start()

    loop(chunks, forward_state)
    acc_sq[...] = jnp.zeros_like(acc_sq)
    acc_cr[...] = jnp.zeros_like(acc_cr)

    def below(first_row, first_col, shape, transposed):
        row = first_row + lax.broadcasted_iota(jnp.int32, shape, 0)
        col = first_col + lax.broadcasted_iota(jnp.int32, shape, 1)
        return (row <= col) if transposed else (row >= col)

    def forward_local(c):
        in_copy(2, c).wait()
        in_copy(3, c).wait()
        for g in range(group):
            cols = hcols(c * group + g)
            for i in range(nblocks):
                mine = pl.ds(i * block, block)
                seen = pl.ds(0, (i + 1) * block)
                s = dot(qb[mine, cols], kb[seen, cols], 1, 1)
                s = jnp.where(below(i * block, 0, s.shape, False), s, 0.0).astype(BF16)
                attb[mine, cols] = dot(s, vb[seen, cols], 1, 0)

    def forward_finish(c):
        for g in range(group):
            cols = hcols(c * group + g)
            att = attb[:, cols] + dot(qb[:, cols], flow[c, g], 1, 0)
            attb[:, cols] = att
            scaled = cb[:, cols].astype(F32) * gain_ref[:, cols]
            acc_sq[...] += att * att
            acc_cr[...] += att * scaled

    first_z = z == 0
    last_z = z == outer - 1
    f_skew = jnp.minimum(1 + 2 * z, chunks)

    def forward_slot(s):
        @pl.when(s < chunks)
        def _():
            forward_local(s)

        c = s - f_skew

        @pl.when(jnp.logical_and(c >= 0, c < chunks))
        def _():
            relay(c, 1, fy, fys, fyr, fzin, fzout, fzs, fzr, flow, first_z, last_z)
            forward_finish(c)

    loop(chunks + f_skew, forward_slot)

    upper = lax.broadcasted_iota(jnp.int32, (8, HD), 0) < 4
    pick_sq = upper.astype(F32)
    pick_cr = 1.0 - pick_sq

    def rowsum(pick, acc):
        return lax.dot_general(
            pick, acc[...], (((1,), (1,)), ((), ())),
            precision=lax.Precision.HIGHEST, preferred_element_type=F32)

    tpb[mt] = rowsum(pick_sq, acc_sq) + rowsum(pick_cr, acc_cr)

    def tp_send(r):
        peer = (mt + r) % ntp
        return pltpu.make_async_remote_copy(
            src_ref=tpb.at[mt], dst_ref=tpb.at[mt], send_sem=tps.at[peer], recv_sem=tpr.at[mt],
            device_id={"tp": peer}, device_id_type=MESH)

    def tp_recv(r):
        peer = (mt + r) % ntp
        return pltpu.make_async_remote_copy(
            src_ref=tpb.at[peer], dst_ref=tpb.at[peer], send_sem=tps.at[peer], recv_sem=tpr.at[peer],
            device_id={"tp": peer}, device_id_type=MESH)

    for r in range(1, ntp):
        tp_send(r).start()
    for r in range(1, ntp):
        tp_recv(r).wait_recv()
    total = tpb[0]
    for i in range(1, ntp):
        total = total + tpb[i]
    inv_row = lax.rsqrt(total[0:1, :] / full_width + epsilon)
    coef_row = inv_row * inv_row * inv_row * total[4:5, :] / full_width
    half = lax.broadcasted_iota(jnp.int32, (8, rows), 0) < 4
    both = jnp.transpose(jnp.where(half, inv_row, coef_row))
    inv_b[...] = jnp.broadcast_to(both[:, 0:1], (rows, HD))
    coef_b[...] = jnp.broadcast_to(both[:, 4:5], (rows, HD))

    def backward_state(c):
        for g in range(group):
            h = c * group + g
            cols = hcols(h)
            inv = inv_b[...]
            gain = gain_ref[:, cols]
            att = attb[:, cols]
            grad = cb[:, cols].astype(F32)
            gout = (grad * gain * inv - att * coef_b[...]).astype(BF16)
            goutb[:, cols] = gout
            by[y, c, g] = dot(qb[:, cols], gout, 0, 0).astype(BF16)
            unit = att * inv
            nst[:, cols] = (unit * gain).astype(BF16)
            ggb[me, pl.ds(h, 1), :] = jnp.sum(grad * unit, axis=0, keepdims=True)
        for r in range(1, inner):
            row_send(c, r, by, bys, byr).start()
        out_copy(0, c).start()

    loop(chunks, backward_state)

    def gg_send(peer):
        return pltpu.make_async_remote_copy(
            src_ref=ggb.at[me], dst_ref=ggb.at[me], send_sem=ggs.at[peer], recv_sem=ggr.at[me],
            device_id={"seq": peer}, device_id_type=MESH)

    def gg_recv(peer):
        return pltpu.make_async_remote_copy(
            src_ref=ggb.at[peer], dst_ref=ggb.at[peer], send_sem=ggs.at[peer], recv_sem=ggr.at[peer],
            device_id={"seq": peer}, device_id_type=MESH)

    loop(n - 1, lambda r: gg_send((me + 1 + r) % n).start())

    def backward_local(c):
        for g in range(group):
            cols = hcols(c * group + g)
            for i in range(nblocks):
                mine = pl.ds(i * block, block)
                seen = pl.ds(0, (i + 1) * block)
                later = pl.ds(i * block, rows - i * block)
                go = goutb[mine, cols]
                b = dot(go, vb[seen, cols], 1, 1)
                b = jnp.where(below(i * block, 0, b.shape, False), b, 0.0).astype(BF16)
                gq = dot(b, kb[seen, cols], 1, 0) + dot(go, flow[c, g], 1, 1)
                qst[mine, cols] = gq.astype(BF16)
                bt = dot(vb[mine, cols], goutb[later, cols], 1, 1)
                keep = below(0, 0, bt.shape, True)
                bt = jnp.where(keep, bt, 0.0).astype(BF16)
                gkb[mine, cols] = dot(bt, qb[later, cols], 1, 0)
                st = dot(kb[mine, cols], qb[later, cols], 1, 1)
                st = jnp.where(keep, st, 0.0).astype(BF16)
                gvb[mine, cols] = dot(st, goutb[later, cols], 1, 0)
        out_copy(1, c).start()

    def backward_finish(c):
        for g in range(group):
            cols = hcols(c * group + g)
            suffix = blow[c, g]
            kst[:, cols] = (gkb[:, cols] + dot(vb[:, cols], suffix, 1, 1)).astype(BF16)
            vst[:, cols] = (gvb[:, cols] + dot(kb[:, cols], suffix, 1, 0)).astype(BF16)
        out_copy(2, c).start()
        out_copy(3, c).start()

    b_skew = jnp.minimum(1 + 2 * (outer - 1 - z), chunks)

    def backward_slot(s):
        @pl.when(s < chunks)
        def _():
            backward_local(s)

        c = s - b_skew

        @pl.when(jnp.logical_and(c >= 0, c < chunks))
        def _():
            relay(c, -1, by, bys, byr, bzin, bzout, bzs, bzr, blow, last_z, first_z)
            backward_finish(c)

    loop(chunks + b_skew, backward_slot)

    loop(n - 1, lambda r: gg_recv((me + 1 + r) % n).wait_recv())
    gain_total = ggb[0]
    for i in range(1, n):
        gain_total = gain_total + ggb[i]
    gg_out[...] = gain_total

    loop(n - 1, lambda r: gg_send((me + 1 + r) % n).wait_send())
    for r in range(1, ntp):
        tp_send(r).wait_send()

    def drain(c):
        for r in range(1, inner):
            row_send(c, r, fy, fys, fyr).wait_send()
            row_send(c, r, by, bys, byr).wait_send()

        @pl.when(jnp.logical_not(last_z))
        def _():
            chain(c, 1, fzin, fzout, fzs, fzr).wait_send()

        @pl.when(jnp.logical_not(first_z))
        def _():
            chain(c, -1, bzin, bzout, bzs, bzr).wait_send()

        for i in range(4):
            out_copy(i, c).wait()

    loop(chunks, drain)


def local(n, ntp, query, key, value, gain, cotangent):
    rows, width = query.shape
    heads = width // HD
    group = 2 if heads % 2 == 0 else 1
    chunks = heads // group
    inner = 1
    while n % (inner * inner * 4) == 0:
        inner *= 2
    state = (chunks, group, HD, HD)
    wide = lambda t: pltpu.VMEM((rows, width), t)
    states = lambda: [
        pltpu.VMEM((inner, *state), BF16), pltpu.VMEM(state, BF16),
        pltpu.VMEM(state, BF16), pltpu.VMEM(state, BF16)]
    dma = pltpu.SemaphoreType.DMA
    sems = lambda: [dma((inner, chunks)), dma((inner, chunks)), dma((chunks,)), dma((chunks,))]
    any_spec = pl.BlockSpec(memory_space=pl.ANY)
    vmem_spec = pl.BlockSpec(memory_space=pltpu.VMEM)
    big = jax.ShapeDtypeStruct((rows, width), BF16)
    outs = pl.pallas_call(
        functools.partial(kernel, n, ntp, inner, group, ntp * width),
        out_shape=[big, big, big, big, jax.ShapeDtypeStruct((heads, HD), F32)],
        in_specs=[any_spec, any_spec, any_spec, vmem_spec, any_spec],
        out_specs=[any_spec, any_spec, any_spec, any_spec, vmem_spec],
        scratch_shapes=[
            wide(BF16), wide(BF16), wide(BF16), wide(BF16),
            wide(F32), wide(BF16), wide(F32), wide(F32),
            wide(BF16), wide(BF16), wide(BF16), wide(BF16),
            *states(), *states(),
            pltpu.VMEM((rows, HD), F32), pltpu.VMEM((rows, HD), F32),
            pltpu.VMEM((rows, HD), F32), pltpu.VMEM((rows, HD), F32),
            pltpu.VMEM((ntp, 8, rows), F32), pltpu.VMEM((n, heads, HD), F32),
            dma((4, chunks)), dma((4, chunks)),
            *sems(), *sems(),
            dma((ntp,)), dma((ntp,)), dma((n,)), dma((n,)),
        ],
        compiler_params=pltpu.CompilerParams(
            collective_id=0, has_side_effects=True, vmem_limit_bytes=60 * 1024 * 1024),
    )(query, key, value, gain.reshape(1, width), cotangent)
    return (*outs[:4], outs[4].reshape(width))


def solution(mesh):
    return jax.shard_map(
        functools.partial(local, mesh.shape["seq"], mesh.shape["tp"]),
        mesh=mesh,
        in_specs=(P("seq", "tp"), P("seq", "tp"), P("seq", "tp"), P("tp"), P("seq", "tp")),
        out_specs=(P("seq", "tp"), P("seq", "tp"), P("seq", "tp"), P("seq", "tp"), P("tp")),
        check_vma=False,
    )
```

time: 240 us -> 83.7 us (0.35)
  waiting for transfers between devices: 88.4 us -> 0 us
  Pallas kernels: 0 us -> 72.9 us
  matrix products: 51.5 us -> 0 us
  blocking collectives: 33.3 us -> 0 us
  local copies, waits for them, and re-layouts: 35 us -> 9.93 us
  other arithmetic: 17.2 us -> 0 us
  between operations: 14.2 us -> 0.65 us
    all_gather x2 -> x0, waiting for transfers between devices: 88.4 us -> none  [the longest x1 63.3 us: local(): shard_rows = lax.all_gather(local_kv[None], 'seq', axis=0, tiled=True)]
    pallas_call x0 -> x1, Pallas kernels: none -> 72.9 us  [local(): pl.pallas_call(functools.partial(kernel, n, ntp, inner, group, ntp * widt...]
    dot_general x12 -> x0, matrix products: 51.5 us -> none  [the longest x1 7.36 us: backward_block(): jnp.einsum('hts,thd->shd', back_low, queries, preferred_element_type=jnp....]
    psum x3 -> x0, blocking collectives: 33.3 us -> none  [the longest x1 20.9 us: local(): grad_gain = lax.psum(gain_part, 'seq')]
    reshape x3 -> x0, local copies, waits for them, and re-layouts: 13.6 us -> none  [the longest x1 5.38 us: local(): attended = attended_blocks.reshape(rows_here, local_width)]
    reduce_sum x3 -> x0, other arithmetic: 10.7 us -> none  [the longest x2 6.55 us: local(): jnp.sum(weight[:, None, None, None] * shard_rows.astype(jnp.float32), axi...]
    unnamed x26 -> x13, local copies, waits for them, and re-layouts: 20.4 us -> 9.93 us
    convert_element_type x3 -> x0, other arithmetic: 6.38 us -> none  [the longest x1 6.37 us: local(): grad_out = grad_out.astype(jnp.bfloat16).reshape(rows_here, head_count, HD)]
  transfers between devices with their start and end apart: 2 -> 0, of which waited for: 2 -> 0; matrix products, arithmetic and copies ran while one was open for 14% -> 0% of each run, Pallas kernels for 0% -> 0%
where the time goes in v1:
time: 83.7 us; the launch traced here: 83.4 us
  Pallas kernels  72.9 us (87%)
  local copies, waits for them, and re-layouts  9.93 us (12%)
    pallas_call x1, Pallas kernels, local(): pl.pallas_call(functools.partial(kernel, n, ntp, inner, group, ntp * widt...  72.9 us
    unnamed x13, local copies, waits for them, and re-layouts  9.93 us

profile of v1, /device:TPU:0, one launch (start us, length us, event | category | flops | bytes accessed | tf_op | source)
XLA Modules:
  0.0 83.4 jit_solution(18037300024971566959)
XLA Ops:
  0.6 72.9 %shard_map.92 = (bf16[512,2048]{1,0:T(8,128)(2,1)}, bf16[512,2048]{1,0:T(8,128)(2,1)}, bf16[512,2048]{1,0:T(8,128)(2,1)}, bf16[512,2048]{1,0:T(8,128)(2,1)}, f32[16,128]{1,0:T(8,128)}) custom-call(bf16[512,2048]{1,0:T(8,128)(2,1)} %q_hbm.1, bf16[512,2048]{1,0:T(8,128)(2,1)} %k_hbm.1, bf16[512,2048]{1,0:T(8,128)(2,1)} %v_hbm.1, f32[1,2048]{1,0:T(1,128)} %bitcast.2, ...), custom_call_target="tpu_custom_call" | custom-call | tf_op jit(solution)/shard_map/pallas_call | solution.py:355
  73.5 0.0 copy-start.2
  73.5 3.3 %copy.15 = bf16[512,2048]{1,0:T(8,128)(2,1)} copy(bf16[512,2048]{1,0:T(8,128)(2,1)} %get-tuple-element.20) | data formatting | bytes 4194304
  76.8 0.0 copy-done.2
  76.8 0.0 copy-start.1
  76.8 1.3 %copy.16 = bf16[512,2048]{1,0:T(8,128)(2,1)} copy(bf16[512,2048]{1,0:T(8,128)(2,1)S(1)} %copy-done.2) | data formatting | bytes 4194304
  78.1 1.0 %copy-done.1 = bf16[512,2048]{1,0:T(8,128)(2,1)S(1)} copy-done((bf16[512,2048]{1,0:T(8,128)(2,1)S(1)}, bf16[512,2048]{1,0:T(8,128)(2,1)}, u32[]{:S(2)}) %copy-start.1) | copy-done | bytes 2097176
  79.2 0.0 copy-start
  79.2 1.3 %copy.17 = bf16[512,2048]{1,0:T(8,128)(2,1)} copy(bf16[512,2048]{1,0:T(8,128)(2,1)S(1)} %copy-done.1) | data formatting | bytes 4194304
  80.5 1.0 %copy-done = bf16[512,2048]{1,0:T(8,128)(2,1)S(1)} copy-done((bf16[512,2048]{1,0:T(8,128)(2,1)S(1)}, bf16[512,2048]{1,0:T(8,128)(2,1)}, u32[]{:S(2)}) %copy-start) | copy-done | bytes 2097176
  81.5 0.0 copy-start.3
  81.5 1.3 %copy.18 = bf16[512,2048]{1,0:T(8,128)(2,1)} copy(bf16[512,2048]{1,0:T(8,128)(2,1)S(1)} %copy-done) | data formatting | bytes 4194304
  82.8 0.0 copy-done.3
  82.8 0.6 copy.19
Async XLA Ops:
  73.5 3.3 %copy-start.2 = (bf16[512,2048]{1,0:T(8,128)(2,1)S(1)}, bf16[512,2048]{1,0:T(8,128)(2,1)}, u32[]{:S(2)}) copy-start(bf16[512,2048]{1,0:T(8,128)(2,1)} %get-tuple-element.21) | copy-start | bytes 6291460
  76.8 2.3 %copy-start.1 = (bf16[512,2048]{1,0:T(8,128)(2,1)S(1)}, bf16[512,2048]{1,0:T(8,128)(2,1)}, u32[]{:S(2)}) copy-start(bf16[512,2048]{1,0:T(8,128)(2,1)} %get-tuple-element.22) | copy-start | bytes 6291460
  79.2 2.3 %copy-start = (bf16[512,2048]{1,0:T(8,128)(2,1)S(1)}, bf16[512,2048]{1,0:T(8,128)(2,1)}, u32[]{:S(2)}) copy-start(bf16[512,2048]{1,0:T(8,128)(2,1)} %get-tuple-element.23) | copy-start | bytes 6291460
  81.5 1.3 %copy-start.3 = (f32[16,128]{1,0:T(8,128)S(1)}, f32[16,128]{1,0:T(8,128)}, u32[]{:S(2)}) copy-start(f32[16,128]{1,0:T(8,128)} %get-tuple-element.14) | copy-start | bytes 24580
